TPU v7x, 32 devices: a whole 2x2x4 slice. The times are simulated.
32 devices in a mesh: rows: 8 (over y, x, core), cores: 4 (over z).
Axes of the slice: x: 2, y: 2, z: 4, core: 2. Of those that a mesh axis runs over, the one named last changes fastest.
Arguments:
- rhs: float32 [131072, 128], P(('rows', 'cores')), may hold values from -6 to 6
- guess: float32 [131072, 128], P(('rows', 'cores')), may hold values from -4 to 4
- degree: float32 [131072], P(('rows', 'cores')), may hold values from 2 to 6
- weights: bfloat16 [1024, 16, 128, 128], P(('rows', 'cores')), may hold values from -0.1875 to 0.1875
- columns: int32 [1024, 16], P(('rows', 'cores')), may hold values from 0 to 95, as said below
- block_counts: int32 [1024], P(('rows', 'cores')), may hold values from 8 to 16, as said below
- send_lists: int32 [32, 32, 2], P(('rows', 'cores')), may hold values from 0 to 31
- aggregates: int32 [131072], P(('rows', 'cores')), may hold values from 0 to 16383
- coarse_diag: float32 [16384], replicated, may hold values from 4 to 32
Outputs:
- smoothed: float32 [131072, 128], P(('rows', 'cores'))
Inputs may be any that keep to these rules, and one draw needn't show every extreme that they name: `block_counts`: every block row has 8 or 16 live slots, and the rows of one device have exactly 320 live slots in all. `columns`: on every device, each table index from 32 up is named by at least one live slot.
All inputs are finite; a program needn't handle non-finite values.
Results may differ from a plain program's by a relative error of at most 0.0022.
Values may be sent and summed in bfloat16 or wider, within the bound.
A program may use at most 128 MiB of HBM per device.

v0:
```python
import functools
import jax
import jax.numpy as jnp
from jax import lax
from jax.experimental import pallas as pl
from jax.experimental.pallas import tpu as pltpu
from jax.sharding import PartitionSpec as P

damping = 0.7
LIMIT = 64 * 1024 * 1024 - 65536
MESH = pl.DeviceIdType.MESH
VM = pl.BlockSpec(memory_space=pltpu.VMEM)
SM = pl.BlockSpec(memory_space=pltpu.SMEM)
ANY = pl.BlockSpec(memory_space=pl.ANY)
f32, bf16, i32 = jnp.float32, jnp.bfloat16, jnp.int32


def column_of(deg, b):
    row = deg[pl.ds(b, 1), :]
    return jnp.transpose(jnp.broadcast_to(row, (row.shape[1], row.shape[1])))


def row_product(w, tab, cols, b):
    slots = w.shape[1]
    left = jnp.concatenate([w[b, s] for s in range(slots)], axis=1)
    right = jnp.concatenate([tab[cols[s, b]] for s in range(slots)], axis=0)
    return jnp.dot(left, right, preferred_element_type=f32)


def each_row(count, step, act):
    @pl.loop(0, count // step)
    def _(i):
        for u in range(step):
            act(i * step + u)


def relax_kernel(nr, nz, guess, rhs_hbm, deg, agg, cols, sends, w_hbm,
                 x1_out, res, tab_out, hagg_out,
                 w, tab1, tab2, pack, aggpack, hagg, dcol, rhs, x1,
                 wsem, bsem, osem, xsem, s1, r1, s2, r2, sa, ra):
    n = nr * nz
    nb = w.shape[0]
    mb = pack.shape[0] // n
    me = lax.axis_index("rows") * nz + lax.axis_index("cores")
    barrier = pltpu.get_barrier_semaphore()

    def where(t):
        return (t // nz, lax.rem(t, nz))

    @pl.loop(1, n)
    def _(k):
        pl.semaphore_signal(barrier, 1, device_id=where(lax.rem(me + k, n)), device_id_type=MESH)

    weights_copy = pltpu.make_async_copy(w_hbm, w, wsem)
    rhs_copy = pltpu.make_async_copy(rhs_hbm, rhs, bsem)
    weights_copy.start()
    rhs_copy.start()

    @pl.loop(0, n)
    def _(t):
        for j in range(mb):
            b = sends[j, t]
            pack[t * mb + j] = guess[b].astype(bf16)
            aggpack[t, pl.ds(j, 1), :] = agg[pl.ds(b, 1), :]

    pl.semaphore_wait(barrier, n - 1)

    def data_copy(k, tab, ss, rr):
        t = lax.rem(me + k, n)
        return pltpu.make_async_remote_copy(
            src_ref=pack.at[pl.ds(t * mb, mb)], dst_ref=tab.at[pl.ds(nb + me * mb, mb)],
            send_sem=ss.at[k], recv_sem=rr.at[k], device_id=where(t), device_id_type=MESH)

    def agg_copy(k):
        t = lax.rem(me + k, n)
        return pltpu.make_async_remote_copy(
            src_ref=aggpack.at[t], dst_ref=hagg.at[me],
            send_sem=sa.at[k], recv_sem=ra.at[k], device_id=where(t), device_id_type=MESH)

    @pl.loop(1, n)
    def _(k):
        data_copy(k, tab1, s1, r1).start()

    @pl.loop(1, n)
    def _(k):
        agg_copy(k).start()

    hagg[me] = aggpack[me]
    for j in range(mb):
        tab1[nb + me * mb + j] = pack[me * mb + j]

    @pl.loop(0, nb)
    def _(b):
        tab1[b] = guess[b].astype(bf16)
        dcol[b] = column_of(deg, b)

    for tab in (tab1, tab2):
        tab[nb + n * mb] = jnp.zeros(tab.shape[1:], bf16)
    weights_copy.wait()
    rhs_copy.wait()

    @pl.loop(1, n)
    def _(k):
        data_copy(k, tab1, s1, r1).wait_recv()

    def sweep(b):
        d, g = dcol[b], guess[b]
        first = g + damping * (rhs[b] - (d * g - row_product(w, tab1, cols, b))) / d
        x1[b] = first
        tab2[b] = first.astype(bf16)

    each_row(nb, 8, sweep)
    x1_copy = pltpu.make_async_copy(x1, x1_out, xsem)
    x1_copy.start()

    @pl.loop(1, n)
    def _(k):
        data_copy(k, tab1, s1, r1).wait_send()
        agg_copy(k).wait()

    @pl.loop(0, n)
    def _(t):
        for j in range(mb):
            pack[t * mb + j] = x1[sends[j, t]].astype(bf16)

    @pl.loop(1, n)
    def _(k):
        data_copy(k, tab2, s2, r2).start()

    for j in range(mb):
        tab2[nb + me * mb + j] = pack[me * mb + j]
    hagg_out[...] = hagg[...]

    @pl.loop(1, n)
    def _(k):
        data_copy(k, tab2, s2, r2).wait_recv()

    out_copy = pltpu.make_async_copy(tab2, tab_out, osem)
    out_copy.start()

    def residue(b):
        res[b] = rhs[b] - (dcol[b] * x1[b] - row_product(w, tab2, cols, b))

    each_row(nb, 8, residue)

    @pl.loop(1, n)
    def _(k):
        data_copy(k, tab2, s2, r2).wait_send()

    out_copy.wait()
    x1_copy.wait()


def restrict_kernel(ways, agg, inv, res, out, *scratch):
    accs, sem = scratch[:ways], scratch[ways]
    for acc in accs:
        acc[...] = jnp.zeros_like(acc)
    span = res.shape[0] // ways
    step = 8

    @pl.loop(0, span // step)
    def _(i):
        for u in range(step):
            places = [agg[q * span + i * step + u] for q in range(ways)]
            sums = [
                accs[q][pl.ds(places[q], 1), :]
                + res[pl.ds(q * span + i * step + u, 1), :] * inv[places[q]]
                for q in range(ways)
            ]
            for q in range(ways):
                accs[q][pl.ds(places[q], 1), :] = sums[q]

    tile, pieces = 64, 8
    piece = out.shape[0] // pieces
    copies = []
    for c in range(pieces):
        @pl.loop(0, piece // tile)
        def _(i):
            rows = pl.ds(c * piece + i * tile, tile)
            total = accs[0][rows, :]
            for acc in accs[1:]:
                total = total + acc[rows, :]
            accs[0][rows, :] = total

        rows = pl.ds(c * piece, piece)
        copy = pltpu.make_async_copy(accs[0].at[rows], out.at[rows], sem.at[c])
        copy.start()
        copies.append(copy)
    for copy in copies:
        copy.wait()


def coarse_kernel(nr, nz, parts, orders, coarse_hbm, out, coarse, acc, sbuf, rbuf, corr, ss, rs, sg, rg, load, store):
    nc = coarse.shape[0]
    top = nc // 2
    r, z = lax.axis_index("rows"), lax.axis_index("cores")
    barrier = pltpu.get_barrier_semaphore()

    def partner(bit):
        axis, m = bit
        other = 1 - 2 * lax.rem((r if axis == 0 else z) // m, 2)
        return (r + other * m, z) if axis == 0 else (r, z + other * m)

    def mine(bit):
        axis, m = bit
        return lax.rem((r if axis == 0 else z) // m, 2)

    every = orders[0]
    count = len(parts)
    base = [sum(parts[:p]) for p in range(count)]
    loads = []
    for side in range(2):
        for p in range(count):
            start = lax.rem(1 - mine(every[0]) + side, 2) * top + base[p]
            rows = pl.ds(pl.multiple_of(start, 16), parts[p])
            copy = pltpu.make_async_copy(coarse_hbm.at[rows], coarse.at[rows], load.at[side * count + p])
            copy.start()
            loads.append(copy)

    for bit in every:
        pl.semaphore_signal(barrier, 1, device_id=partner(bit), device_id_type=MESH)
    pl.semaphore_wait(barrier, len(every))

    levels = len(every)
    room, at = [], 0
    for s in range(levels):
        row = []
        for p in range(count):
            size = parts[p] >> s
            row.append((at, size))
            at += size
        room.append(row)

    def sized(size):
        tile = 64
        while size % tile:
            tile //= 2
        return tile

    def rows_of(start, tile, i):
        return pl.ds(pl.multiple_of(start + i * tile, 16), tile)

    def hop(s, p):
        at, size = room[s][p]
        return pltpu.make_async_remote_copy(
            src_ref=sbuf.at[pl.ds(at, size)], dst_ref=rbuf.at[pl.ds(at, size)],
            send_sem=ss.at[s * count + p], recv_sem=rs.at[s * count + p],
            device_id=partner(orders[p][s]), device_id_type=MESH)

    place = list(base)
    for s in range(levels):
        for p in range(count):
            bit = mine(orders[p][s])
            at, size = room[s][p]
            tile = sized(size)
            if s == 0:
                loads[p].wait()
                keep, give, source = bit * top + base[p], (1 - bit) * top + base[p], coarse
            else:
                old_at, old_size = room[s - 1][p]
                hop(s - 1, p).wait_recv()
                if s == 1:
                    loads[count + p].wait()
                was = place[p]
                keep, give, source = was + bit * size, was + (1 - bit) * size, acc
                held = coarse if s == 1 else acc
                shift = mine(orders[p][0]) * top if s == 1 else 0
                old_tile = sized(old_size)

                @pl.loop(0, old_size // old_tile)
                def _(i):
                    rows = rows_of(was, old_tile, i)
                    acc[rows, :] = held[rows_of(was + shift, old_tile, i), :] + rbuf[
                        rows_of(old_at, old_tile, i), :].astype(f32)

                place[p] = keep

            @pl.loop(0, size // tile)
            def _(i):
                sbuf[rows_of(at, tile, i), :] = source[rows_of(give, tile, i), :].astype(bf16)

            hop(s, p).start()

    def spread(s, p, start):
        size = parts[p] >> s
        rows = pl.ds(pl.multiple_of(start, 16), size)
        return pltpu.make_async_remote_copy(
            src_ref=corr.at[rows], dst_ref=corr.at[rows],
            send_sem=sg.at[s * count + p], recv_sem=rg.at[s * count + p],
            device_id=partner(orders[p][s]), device_id_type=MESH)

    shift = mine(every[0]) * top
    sent = []
    for s in reversed(range(levels)):
        for p in range(count):
            if s == levels - 1:
                hop(s, p).wait_recv()
                at, size = room[s][p]
                tile = sized(size)
                was = place[p]

                @pl.loop(0, size // tile)
                def _(i):
                    corr[rows_of(was + shift, tile, i), :] = (
                        acc[rows_of(was, tile, i), :] + rbuf[rows_of(at, tile, i), :].astype(f32)
                    ).astype(bf16)
            else:
                sent[-count].wait_recv()
                place[p] = place[p] - mine(orders[p][s + 1]) * (parts[p] >> (s + 1))
            copy = spread(s, p, place[p] + shift)
            copy.start()
            sent.append(copy)

    def flush(start, size, index):
        rows = pl.ds(pl.multiple_of(start, 16), size)
        return pltpu.make_async_copy(corr.at[rows], out.at[rows], store.at[index])

    flushes = [flush(shift, top, 0)]
    flushes[0].start()
    for p in range(count):
        sent[p - count].wait_recv()
        flushes.append(flush(top - shift + base[p], parts[p], 1 + p))
        flushes[-1].start()
    for copy in sent:
        copy.wait_send()
    for s in range(levels):
        for p in range(count):
            hop(s, p).wait_send()

    for copy in flushes:
        copy.wait()


def smooth_kernel(corr, agg, hagg, x1tab, x1_hbm, rhs_hbm, deg, cols, w_hbm, out,
                  w, fine, tab, x2, rhs, sems):
    nb, size = w.shape[0], w.shape[2]
    pairs = ((x1tab, tab), (x1_hbm, x2), (w_hbm, w), (rhs_hbm, rhs))
    copies = [pltpu.make_async_copy(a, b, sems.at[k]) for k, (a, b) in enumerate(pairs)]
    for copy in copies:
        copy.start()

    @pl.loop(0, corr.shape[0] // 128)
    def _(i):
        rows = pl.ds(i * 128, 128)
        fine[rows, :] = corr[rows, :].astype(f32)

    copies[0].wait()
    copies[1].wait()
    step = 16

    def gathered(ids, first):
        return jnp.concatenate([fine[pl.ds(ids[first + u], 1), :] for u in range(step)], axis=0)

    @pl.loop(0, nb)
    def _(b):
        for i in range(size // step):
            rows = slice(i * step, (i + 1) * step)
            second = x2[b, rows, :] + gathered(agg, b * size + i * step)
            x2[b, rows, :] = second
            tab[b, rows, :] = second.astype(bf16)

    @pl.loop(nb, tab.shape[0] - 1)
    def _(b):
        for i in range(size // step):
            rows = slice(i * step, (i + 1) * step)
            moved = tab[b, rows, :].astype(f32) + gathered(hagg, (b - nb) * size + i * step)
            tab[b, rows, :] = moved.astype(bf16)

    copies[2].wait()
    copies[3].wait()

    def finish(b):
        d, second = column_of(deg, b), x2[b]
        out[b] = second + damping * (rhs[b] - (d * second - row_product(w, tab, cols, b))) / d

    each_row(nb, 8, finish)


def halve_orders(nr, nz):
    row_bits = [(0, 1 << k) for k in range(1, nr.bit_length() - 1)]
    z_bits = [(1, 1 << k) for k in range(nz.bit_length() - 1)]
    core = [(0, 1)]
    return 2 * [
        core + row_bits[:1] + z_bits[:1] + row_bits[1:] + z_bits[1:],
        core + row_bits[::-1] + z_bits,
        core + z_bits + row_bits,
    ]


def body(nr, nz, rhs, guess, degree, weights, columns, block_counts, send_lists, aggregates, coarse_diag):
    n = nr * nz
    nb, slots, bs = weights.shape[0], weights.shape[1], weights.shape[2]
    width = rhs.shape[1]
    nc = coarse_diag.shape[0]
    mb = send_lists.shape[2]
    nt = nb + n * mb + 1
    dma = pltpu.SemaphoreType.DMA
    rhs3, guess3 = rhs.reshape(nb, bs, width), guess.reshape(nb, bs, width)
    deg2, agg2 = degree.reshape(nb, bs), aggregates.reshape(nb, bs)
    live = jnp.arange(slots, dtype=i32)[:, None] < block_counts[None, :]
    cols = jnp.where(live, columns.T, nt - 1)
    field = jax.ShapeDtypeStruct((nb, bs, width), f32)

    x1, res, x1tab, hagg = pl.pallas_call(
        functools.partial(relax_kernel, nr, nz),
        out_shape=(field, field, jax.ShapeDtypeStruct((nt, bs, width), bf16),
                   jax.ShapeDtypeStruct((n, mb, bs), i32)),
        in_specs=[VM, ANY, VM, VM, SM, SM, ANY],
        out_specs=(ANY, VM, ANY, VM),
        scratch_shapes=[
            pltpu.VMEM((nb, slots, bs, bs), bf16),
            pltpu.VMEM((nt, bs, width), bf16),
            pltpu.VMEM((nt, bs, width), bf16),
            pltpu.VMEM((n * mb, bs, width), bf16),
            pltpu.VMEM((n, mb, bs), i32),
            pltpu.VMEM((n, mb, bs), i32),
            pltpu.VMEM((nb, bs, width), f32),
            pltpu.VMEM((nb, bs, width), f32),
            pltpu.VMEM((nb, bs, width), f32),
            dma, dma, dma, dma, dma((n,)), dma((n,)), dma((n,)), dma((n,)), dma((n,)), dma((n,)),
        ],
        compiler_params=pltpu.CompilerParams(
            collective_id=1, has_side_effects=True, vmem_limit_bytes=LIMIT),
        name="relax",
    )(guess3, rhs3, deg2, agg2, cols, send_lists[0].T, weights)

    ways = 4
    local_coarse = pl.pallas_call(
        functools.partial(restrict_kernel, ways),
        out_shape=jax.ShapeDtypeStruct((nc, width), f32),
        in_specs=[SM, SM, VM],
        out_specs=ANY,
        scratch_shapes=[pltpu.VMEM((nc, width), f32)] * ways + [dma((8,))],
        compiler_params=pltpu.CompilerParams(vmem_limit_bytes=LIMIT),
        name="restrict",
    )(aggregates, 1.0 / coarse_diag, res.reshape(nb * bs, width))

    orders = halve_orders(nr, nz)
    top = nc // 2
    unit = 16 * (n // 2)
    units = top // unit
    count = len(orders)
    parts = [(units + count - 1 - p) // count * unit for p in range(count)]
    levels = len(orders[0])
    moved = sum(size >> s for s in range(levels) for size in parts)
    sems = dma((levels * count,))
    correction = pl.pallas_call(
        functools.partial(coarse_kernel, nr, nz, parts, orders),
        out_shape=jax.ShapeDtypeStruct((nc, width), bf16),
        in_specs=[ANY],
        out_specs=ANY,
        scratch_shapes=[
            pltpu.VMEM((nc, width), f32),
            pltpu.VMEM((top, width), f32),
            pltpu.VMEM((moved, width), bf16),
            pltpu.VMEM((moved, width), bf16),
            pltpu.VMEM((nc, width), bf16),
            sems, sems, sems, sems, dma((2 * count,)), dma((count + 1,)),
        ],
        compiler_params=pltpu.CompilerParams(
            collective_id=2, has_side_effects=True, vmem_limit_bytes=LIMIT),
        name="coarse",
    )(local_coarse)

    out = pl.pallas_call(
        smooth_kernel,
        out_shape=field,
        in_specs=[VM, SM, SM, ANY, ANY, ANY, VM, SM, ANY],
        out_specs=VM,
        scratch_shapes=[
            pltpu.VMEM((nb, slots, bs, bs), bf16),
            pltpu.VMEM((nc, width), f32),
            pltpu.VMEM((nt, bs, width), bf16),
            pltpu.VMEM((nb, bs, width), f32),
            pltpu.VMEM((nb, bs, width), f32),
            dma((4,)),
        ],
        compiler_params=pltpu.CompilerParams(vmem_limit_bytes=LIMIT),
        name="smooth",
    )(correction, aggregates, hagg.reshape(-1), x1tab, x1, rhs3, deg2, cols, weights)
    return out.reshape(nb * bs, width)


def solution(mesh):
    both = ("rows", "cores")
    return jax.shard_map(
        functools.partial(body, mesh.shape["rows"], mesh.shape["cores"]),
        mesh=mesh,
        in_specs=(
            P(both, None), P(both, None), P(both), P(both, None, None, None), P(both, None),
            P(both), P(both, None, None), P(both), P(),
        ),
        out_specs=P(both, None),
        check_vma=False,
    )
```

profile of v0, /device:TPU:1, one launch (start us, length us, event | category | flops | bytes accessed | tf_op | source)
XLA Modules:
  0.0 206.5 jit_solution(17690944471742402466)
XLA Ops:
  0.0 1.3 bitcast_select_fusion.cols
  1.3 1.5 broadcast_divide_fusion.inv
  2.8 114.7 %relax.1 = (f32[32,128,128]{2,1,0:T(8,128)}, f32[32,128,128]{2,1,0:T(8,128)}, bf16[97,128,128]{2,1,0:T(8,128)(2,1)}, s32[32,2,128]{2,1,0:T(2,128)}) custom-call(f32[32,128,128]{2,1,0:T(8,128)} %bitcast.14, f32[32,128,128]{2,1,0:T(8,128)} %bitcast.12, f32[32,128]{1,0:T(8,128)} %bitcast.17, s32[32,128]{1,0:T(8,128)} %bitcast.16, ...), custom_call_target="tpu_custom_call" | custom-call | tf_op jit(solution)/shard_map/relax/pallas_call | solution.py:404
  117.5 13.9 %restrict.1.coarse_hbm = f32[16384,128]{1,0:T(8,128)} custom-call(s32[4096]{0:T(1024)} %agg.3, f32[16384]{0:T(1024)} %broadcast_divide_fusion.inv, f32[4096,128]{1,0:T(8,128)} %bitcast.15), custom_call_target="tpu_custom_call" | custom-call | tf_op jit(solution)/shard_map/restrict/pallas_call | solution.py:428
  131.4 53.3 %coarse.1.corr = bf16[16384,128]{1,0:T(8,128)(2,1)} custom-call(f32[16384,128]{1,0:T(8,128)} %restrict.1.coarse_hbm), custom_call_target="tpu_custom_call" | custom-call | tf_op jit(solution)/shard_map/coarse/pallas_call | solution.py:447
  184.8 21.7 %smooth.1 = f32[32,128,128]{2,1,0:T(8,128)} custom-call(bf16[16384,128]{1,0:T(8,128)(2,1)} %coarse.1.corr, s32[4096]{0:T(1024)} %agg.3, s32[8192]{0:T(1024)} %bitcast.19, bf16[97,128,128]{2,1,0:T(8,128)(2,1)} %get-tuple-element.11.x1tab, f32[32,128,128]{2,1,0:T(8,128)} %get-tuple-element.12.x1_hbm, f32[32,128,128]{2,1,0:T(8,128)} %bitcast.13, ...), custom_call_target="tpu_custom_call" | custom-call | tf_op jit(solution)/shard_map/smooth/pallas_call | solution.py:465
where the time goes:
time: 207 us
  Pallas kernels  204 us (99%)
  other arithmetic  2.77 us (1%)
    pallas_call x1, Pallas kernels, body(): pl.pallas_call(functools.partial(relax_kernel, nr, nz), out_shape=(field,...  115 us
    pallas_call x1, Pallas kernels, body(): pl.pallas_call(functools.partial(coarse_kernel, nr, nz, parts, orders), o...  53.3 us
    pallas_call x1, Pallas kernels, body(): pl.pallas_call(smooth_kernel, out_shape=field, in_specs=[VM, SM, SM, ANY,...  21.7 us
    pallas_call x1, Pallas kernels, body(): pl.pallas_call(functools.partial(restrict_kernel, ways), out_shape=jax.Sh...  13.9 us

commit v1 on v0

v1 whole, which is shorter than its diff:
```python
import functools
import jax
import jax.numpy as jnp
from jax import lax
from jax.experimental import pallas as pl
from jax.experimental.pallas import tpu as pltpu
from jax.sharding import PartitionSpec as P

damping = 0.7
MIB = 1024 * 1024
LIMIT = 64 * 1024 * 1024 - 65536
MESH = pl.DeviceIdType.MESH
VM = pl.BlockSpec(memory_space=pltpu.VMEM)
SM = pl.BlockSpec(memory_space=pltpu.SMEM)
ANY = pl.BlockSpec(memory_space=pl.ANY)
f32, bf16, i32 = jnp.float32, jnp.bfloat16, jnp.int32


def column_of(deg, b):
    row = deg[pl.ds(b, 1), :]
    return jnp.transpose(jnp.broadcast_to(row, (row.shape[1], row.shape[1])))


def row_product(w, tab, cols, b, first, count):
    left = jnp.concatenate([w[b, first + s] for s in range(count)], axis=1)
    right = jnp.concatenate([tab[cols[first + s, b]] for s in range(count)], axis=0)
    return jnp.dot(left, right, preferred_element_type=f32)


def find_full_rows(counts, half, pick, spot):
    nb, extra = spot.shape[0], pick.shape[0]

    def look(b, found):
        rank, rows = found[0], found[1:]
        full = jnp.where(counts[b] > half, 1, 0)
        spot[b] = jnp.where(full == 1, rank, extra)
        rows = [row + jnp.where(rank == e, full * b, 0) for e, row in enumerate(rows)]
        return (rank + full, *rows)

    zero = jnp.zeros((), i32)
    found = lax.fori_loop(0, nb, look, (zero,) * (extra + 1))
    for e in range(extra):
        pick[e] = found[1 + e]


def full_products(w, tab, cols, half, pick, ex):
    for e in range(pick.shape[0]):
        ex[e] = row_product(w, tab, cols, pick[e], half, half)


def vmem(x):
    return pltpu.with_memory_space_constraint(x, pltpu.VMEM)


def each_row(count, step, act):
    @pl.loop(0, count // step)
    def _(i):
        for u in range(step):
            act(i * step + u)


def relax_kernel(nr, nz, guess, rhs_hbm, deg, agg, cols, counts, sends, w_hbm,
                 x1_out, res, ids_out,
                 w, tab1, tab2, pack, aggpack, hagg, dcol, rhs, x1, ex, pick, spot,
                 wsem, bsem, xsem, s1, r1, s2, r2, sa, ra):
    n = nr * nz
    nb, half = w.shape[0], w.shape[1] // 2
    mb = pack.shape[0] // n
    me = lax.axis_index("rows") * nz + lax.axis_index("cores")
    barrier = pltpu.get_barrier_semaphore()

    def where(t):
        return (t // nz, lax.rem(t, nz))

    @pl.loop(1, n)
    def _(k):
        pl.semaphore_signal(barrier, 1, device_id=where(lax.rem(me + k, n)), device_id_type=MESH)

    weights_copy = pltpu.make_async_copy(w_hbm, w, wsem)
    rhs_copy = pltpu.make_async_copy(rhs_hbm, rhs, bsem)
    weights_copy.start()
    rhs_copy.start()

    @pl.loop(0, n)
    def _(t):
        for j in range(mb):
            b = sends[j, t]
            pack[t * mb + j] = guess[b].astype(bf16)
            aggpack[t, pl.ds(j, 1), :] = agg[pl.ds(b, 1), :]

    pl.semaphore_wait(barrier, n - 1)

    def data_copy(k, tab, ss, rr):
        t = lax.rem(me + k, n)
        return pltpu.make_async_remote_copy(
            src_ref=pack.at[pl.ds(t * mb, mb)], dst_ref=tab.at[pl.ds(nb + me * mb, mb)],
            send_sem=ss.at[k], recv_sem=rr.at[k], device_id=where(t), device_id_type=MESH)

    def agg_copy(k):
        t = lax.rem(me + k, n)
        return pltpu.make_async_remote_copy(
            src_ref=aggpack.at[t], dst_ref=hagg.at[me],
            send_sem=sa.at[k], recv_sem=ra.at[k], device_id=where(t), device_id_type=MESH)

    @pl.loop(1, n)
    def _(k):
        data_copy(k, tab1, s1, r1).start()

    @pl.loop(1, n)
    def _(k):
        agg_copy(k).start()

    hagg[me] = aggpack[me]
    for j in range(mb):
        tab1[nb + me * mb + j] = pack[me * mb + j]

    @pl.loop(0, nb)
    def _(b):
        tab1[b] = guess[b].astype(bf16)
        dcol[b] = column_of(deg, b)

    find_full_rows(counts, half, pick, spot)
    ex[pick.shape[0]] = jnp.zeros(ex.shape[1:], f32)
    weights_copy.wait()
    rhs_copy.wait()

    @pl.loop(1, n)
    def _(k):
        data_copy(k, tab1, s1, r1).wait_recv()

    def sweep(b):
        d, g = dcol[b], guess[b]
        off = row_product(w, tab1, cols, b, 0, half) + ex[spot[b]]
        first = g + damping * (rhs[b] - (d * g - off)) / d
        x1[b] = first
        tab2[b] = first.astype(bf16)

    full_products(w, tab1, cols, half, pick, ex)
    each_row(nb, 8, sweep)
    x1_copy = pltpu.make_async_copy(x1, x1_out, xsem)
    x1_copy.start()

    @pl.loop(1, n)
    def _(k):
        data_copy(k, tab1, s1, r1).wait_send()
        agg_copy(k).wait()

    @pl.loop(0, n)
    def _(t):
        for j in range(mb):
            pack[t * mb + j] = x1[sends[j, t]].astype(bf16)

    @pl.loop(1, n)
    def _(k):
        data_copy(k, tab2, s2, r2).start()

    for j in range(mb):
        tab2[nb + me * mb + j] = pack[me * mb + j]
    ids_out[pl.ds(0, nb), :] = agg[...]

    @pl.loop(0, n)
    def _(t):
        ids_out[pl.ds(nb + t * mb, mb), :] = hagg[t]


    @pl.loop(1, n)
    def _(k):
        data_copy(k, tab2, s2, r2).wait_recv()

    def residue(b):
        off = row_product(w, tab2, cols, b, 0, half) + ex[spot[b]]
        res[b] = rhs[b] - (dcol[b] * x1[b] - off)

    full_products(w, tab2, cols, half, pick, ex)
    each_row(nb, 8, residue)

    @pl.loop(1, n)
    def _(k):
        data_copy(k, tab2, s2, r2).wait_send()

    x1_copy.wait()


def restrict_kernel(ways, agg, res, keep, give, *accs):
    for acc in accs:
        acc[...] = jnp.zeros_like(acc)
    span = res.shape[0] // ways
    step = 8

    @pl.loop(0, span // step)
    def _(i):
        for u in range(step):
            places = [agg[q * span + i * step + u] for q in range(ways)]
            sums = [
                accs[q][pl.ds(places[q], 1), :] + res[pl.ds(q * span + i * step + u, 1), :]
                for q in range(ways)
            ]
            for q in range(ways):
                accs[q][pl.ds(places[q], 1), :] = sums[q]

    top = keep.shape[0]
    bit = lax.rem(lax.axis_index("rows"), 2)
    tile = 64

    def total(start):
        rows = pl.ds(pl.multiple_of(start, 16), tile)
        value = accs[0][rows, :]
        for acc in accs[1:]:
            value = value + acc[rows, :]
        return value

    @pl.loop(0, top // tile)
    def _(i):
        rows = pl.ds(i * tile, tile)
        give[rows, :] = total((1 - bit) * top + i * tile).astype(bf16)
        keep[rows, :] = total(bit * top + i * tile)


def cycle_kernel(parts, stages, give, keep, diag, x1_hbm, res, deg, ids_hbm, cols, counts, w_hbm, out,
                 w, first, sbuf, rbuf, corr, fine, tab, ex, base, dcol, dinv, turned, ids, pick, spot,
                 ss, rs, sg, rg, more):
    top = keep.shape[0]
    acc = fine
    nb, half, size = w.shape[0], w.shape[1] // 2, w.shape[2]
    r, z = lax.axis_index("rows"), lax.axis_index("cores")
    barrier = pltpu.get_barrier_semaphore()
    count = len(parts)
    begin = [sum(parts[:p]) for p in range(count)]

    def mine(bit):
        axis, m = bit
        return lax.rem((r if axis == 0 else z) // m, 2)

    def peer(bits, d):
        at, index = [r, z], 0
        for i, bit in enumerate(bits):
            flip = (d >> (len(bits) - 1 - i)) & 1
            b = mine(bit)
            if flip:
                at[bit[0]] = at[bit[0]] + (1 - 2 * b) * bit[1]
                b = 1 - b
            index = index * 2 + b
        return tuple(at), index

    def rows_of(start, tile, i):
        return pl.ds(pl.multiple_of(start + i * tile, 16), tile)

    def tiled(rows, act):
        tile = 64
        while rows % tile:
            tile //= 2

        @pl.loop(0, rows // tile)
        def _(i):
            act(tile, i)

    met = []
    for order in stages:
        for bits in order:
            for d in range(1, 1 << len(bits)):
                key = tuple(sorted(bit for i, bit in enumerate(bits) if (d >> (len(bits) - 1 - i)) & 1))
                if key not in met:
                    met.append(key)
                    pl.semaphore_signal(barrier, 1, device_id=peer(bits, d)[0], device_id_type=MESH)
    pairs = ((ids_hbm, ids), (x1_hbm, base), (w_hbm, w))
    others = [pltpu.make_async_copy(a, b, more.at[k]) for k, (a, b) in enumerate(pairs)]
    others[0].start()
    others[1].start()
    pl.semaphore_wait(barrier, len(met))

    room, slots, at, taken = {}, {}, 0, 0
    for p in range(count):
        left = parts[p]
        for s, bits in enumerate(stages[p]):
            group = 1 << len(bits)
            if s:
                left //= group
            for d in range(1, group):
                slots[p, s, d] = taken
                taken += 1
                if s:
                    room[p, s, d] = (at, left)
                    at += left

    def hop(p, s, d):
        k = slots[p, s, d]
        if s == 0:
            rows = pl.ds(begin[p], parts[p])
            source, target = give.at[rows], first.at[rows]
        else:
            at, left = room[p, s, d]
            rows = pl.ds(at, left)
            source, target = sbuf.at[rows], rbuf.at[rows]
        return pltpu.make_async_remote_copy(
            src_ref=source, dst_ref=target, send_sem=ss.at[k], recv_sem=rs.at[k],
            device_id=peer(stages[p][s], d)[0], device_id_type=MESH)

    for p in range(count):
        hop(p, 0, 1).start()

    find_full_rows(counts, half, pick, spot)
    ex[pick.shape[0]] = jnp.zeros(ex.shape[1:], f32)
    shift = mine(stages[0][0][0]) * top

    def place_of(p):
        place, left = begin[p], parts[p]
        for bits in stages[p][1:]:
            left //= 1 << len(bits)
            place = place + peer(bits, 0)[1] * left
        return place, left

    final = 0
    spots = []
    for p in range(count):
        place, left = place_of(p)
        spots.append(final)

        @pl.loop(0, left // 16)
        def _(i):
            start = shift + place + i * 16
            turned[...] = column_of(diag, start // 128)
            dinv[pl.ds(spots[p] + i * 16, 16), :] = 1.0 / turned[pl.ds(pl.multiple_of(lax.rem(start, 128), 16), 16), :]

        final += left

    def gathered(p, s, start, rows):
        def add(tile, i):
            here = rows_of(start, tile, i)
            if s == 0:
                acc[here, :] = keep[here, :] + first[here, :].astype(f32)
            else:
                total = acc[here, :]
                for d in range(1, 1 << len(stages[p][s])):
                    total = total + rbuf[rows_of(room[p, s, d][0], tile, i), :].astype(f32)
                acc[here, :] = total

        tiled(rows, add)

    regions = list(begin)
    sizes = list(parts)
    levels = max(len(order) for order in stages)
    for s in range(1, levels):
        for p in range(count):
            if s >= len(stages[p]):
                continue
            for d in range(1, 1 << len(stages[p][s - 1])):
                hop(p, s - 1, d).wait_recv()
            gathered(p, s - 1, regions[p], sizes[p])
            bits = stages[p][s]
            left = sizes[p] >> len(bits)
            for d in range(1, 1 << len(bits)):
                start = regions[p] + peer(bits, d)[1] * left
                at = room[p, s, d][0]

                def send(tile, i):
                    sbuf[rows_of(at, tile, i), :] = acc[rows_of(start, tile, i), :].astype(bf16)

                tiled(left, send)
                hop(p, s, d).start()
            regions[p], sizes[p] = regions[p] + peer(bits, 0)[1] * left, left
        if s == 1:
            others[2].start()

            @pl.loop(0, nb)
            def _(b):
                dcol[b] = damping / column_of(deg, b)

            others[1].wait()

            @pl.loop(0, nb)
            def _(b):
                base[b] = base[b] + dcol[b] * res[b]

    def spread(p, s, d, start, left):
        rows = pl.ds(pl.multiple_of(start, 16), left)
        k = slots[p, s, d]
        return pltpu.make_async_remote_copy(
            src_ref=corr.at[rows], dst_ref=corr.at[rows], send_sem=sg.at[k], recv_sem=rg.at[k],
            device_id=peer(stages[p][s], d)[0], device_id_type=MESH)

    def widen(start, rows):
        def act(tile, i):
            fine[rows_of(start, tile, i), :] = corr[rows_of(start, tile, i), :].astype(f32)
        tiled(rows, act)

    sent, waits = [], {}
    for s in reversed(range(levels)):
        for p in range(count):
            last = len(stages[p]) - 1
            if s > last:
                continue
            if s == last:
                for d in range(1, 1 << len(stages[p][s])):
                    hop(p, s, d).wait_recv()
                start, left = regions[p], sizes[p]
                gathered(p, s, start, left)

                def settle(tile, i):
                    corr[rows_of(shift + start, tile, i), :] = (
                        acc[rows_of(start, tile, i), :] * dinv[rows_of(spots[p], tile, i), :]).astype(bf16)

                tiled(left, settle)
            else:
                for copy in waits[p]:
                    copy.wait_recv()
                bits = stages[p][s + 1]
                regions[p] = regions[p] - peer(bits, 0)[1] * sizes[p]
                sizes[p] = sizes[p] << len(bits)
            waits[p] = [
                spread(p, s, d, shift + regions[p], sizes[p]) for d in range(1, 1 << len(stages[p][s]))
            ]
            for copy in waits[p]:
                copy.start()
            sent += waits[p]
            if s == 0:
                widen(shift + begin[p], parts[p])
    others[0].wait()
    for p in range(count):
        for copy in waits[p]:
            copy.wait_recv()
        widen(top - shift + begin[p], parts[p])

    step = 16

    @pl.loop(0, tab.shape[0])
    def _(b):
        for i in range(size // step):
            tab[b, i * step:(i + 1) * step, :] = jnp.concatenate(
                [fine[pl.ds(ids[b * size + i * step + u], 1), :] for u in range(step)], axis=0).astype(bf16)

    others[2].wait()
    full_products(w, tab, cols, half, pick, ex)

    def finish(b):
        off = row_product(w, tab, cols, b, 0, half) + ex[spot[b]]
        out[b] = base[b] + (1.0 - damping) * tab[b].astype(f32) + dcol[b] * off

    each_row(nb, 8, finish)
    for copy in sent:
        copy.wait_send()
    for p, s, d in slots:
        hop(p, s, d).wait_send()


def stage_plan(nr, nz):
    row_bits = [((0, 1 << k),) for k in range(1, nr.bit_length() - 1)]
    z_bits = [(1, 1 << k) for k in range(nz.bit_length() - 1)]
    core = [((0, 1),)]
    swapped = row_bits[::-1]
    apart, together = [(bit,) for bit in z_bits], [tuple(z_bits)]
    a = core + row_bits + together
    b = core + swapped + together
    c = core + apart + row_bits
    d = core + apart + swapped
    return [(c, 2), (d, 2), (a, 6), (b, 6), (c, 2), (d, 2), (a, 6), (b, 6)]


def body(nr, nz, rhs, guess, degree, weights, columns, block_counts, send_lists, aggregates, coarse_diag):
    n = nr * nz
    nb, slots, bs = weights.shape[0], weights.shape[1], weights.shape[2]
    width = rhs.shape[1]
    nc = coarse_diag.shape[0]
    mb = send_lists.shape[2]
    nt = nb + n * mb
    extra = nb // 4
    dma = pltpu.SemaphoreType.DMA
    rhs3, guess3 = rhs.reshape(nb, bs, width), guess.reshape(nb, bs, width)
    deg2, agg2 = degree.reshape(nb, bs), aggregates.reshape(nb, bs)
    field = jax.ShapeDtypeStruct((nb, bs, width), f32)

    x1, res, ids = pl.pallas_call(
        functools.partial(relax_kernel, nr, nz),
        out_shape=(field, pltpu.VMEM((nb, bs, width), f32), jax.ShapeDtypeStruct((nt, bs), i32)),
        in_specs=[VM, ANY, VM, VM, SM, SM, SM, ANY],
        out_specs=(ANY, VM, VM),
        scratch_shapes=[
            pltpu.VMEM((nb, slots, bs, bs), bf16),
            pltpu.VMEM((nt, bs, width), bf16),
            pltpu.VMEM((nt, bs, width), bf16),
            pltpu.VMEM((n * mb, bs, width), bf16),
            pltpu.VMEM((n, mb, bs), i32),
            pltpu.VMEM((n, mb, bs), i32),
            pltpu.VMEM((nb, bs, width), f32),
            pltpu.VMEM((nb, bs, width), f32),
            pltpu.VMEM((nb, bs, width), f32),
            pltpu.VMEM((extra + 1, bs, width), f32),
            pltpu.SMEM((extra,), i32), pltpu.SMEM((nb,), i32),
            dma, dma, dma, dma((n,)), dma((n,)), dma((n,)), dma((n,)), dma((n,)), dma((n,)),
        ],
        compiler_params=pltpu.CompilerParams(
            collective_id=1, has_side_effects=True, vmem_limit_bytes=54 * MIB),
        name="relax",
    )(guess3, rhs3, deg2, agg2, columns.T, block_counts, send_lists[0].T, weights)

    ways = 4
    top = nc // 2
    keep, give = pl.pallas_call(
        functools.partial(restrict_kernel, ways),
        out_shape=(pltpu.VMEM((top, width), f32), pltpu.VMEM((top, width), bf16)),
        in_specs=[SM, VM],
        out_specs=(VM, VM),
        scratch_shapes=[pltpu.VMEM((nc, width), f32)] * ways,
        compiler_params=pltpu.CompilerParams(vmem_limit_bytes=36 * MIB),
        name="restrict",
    )(aggregates, vmem(res.reshape(nb * bs, width)))

    plan = stage_plan(nr, nz)
    stages = [order for order, _ in plan]
    unit = 16 * (n // 2)
    units = top // unit
    whole = sum(weight for _, weight in plan)
    marks = [units * sum(weight for _, weight in plan[:p]) // whole for p in range(len(plan) + 1)]
    parts = [(hi - lo) * unit for lo, hi in zip(marks, marks[1:])]
    stages = [order for order, part in zip(stages, parts) if part]
    parts = [part for part in parts if part]
    hops, moved = 0, 0
    for order, left in zip(stages, parts):
        for s, bits in enumerate(order):
            group = 1 << len(bits)
            hops += group - 1
            if s:
                left //= group
                moved += (group - 1) * left
    out = pl.pallas_call(
        functools.partial(cycle_kernel, parts, stages),
        out_shape=pltpu.VMEM((nb, bs, width), f32),
        in_specs=[VM, VM, VM, ANY, VM, VM, ANY, SM, SM, ANY],
        out_specs=VM,
        scratch_shapes=[
            pltpu.VMEM((nb, slots, bs, bs), bf16),
            pltpu.VMEM((top, width), bf16),
            pltpu.VMEM((moved, width), bf16),
            pltpu.VMEM((moved, width), bf16),
            pltpu.VMEM((nc, width), bf16),
            pltpu.VMEM((nc, width), f32),
            pltpu.VMEM((nt, bs, width), bf16),
            pltpu.VMEM((extra + 1, bs, width), f32),
            pltpu.VMEM((nb, bs, width), f32),
            pltpu.VMEM((nb, bs, width), f32),
            pltpu.VMEM((top // (n // 2), width), f32),
            pltpu.VMEM((bs, width), f32),
            pltpu.SMEM((nt * bs,), i32), pltpu.SMEM((extra,), i32), pltpu.SMEM((nb,), i32),
            dma((hops,)), dma((hops,)), dma((hops,)), dma((hops,)), dma((3,)),
        ],
        compiler_params=pltpu.CompilerParams(
            collective_id=2, has_side_effects=True, vmem_limit_bytes=52 * MIB if nt > 128 else 46 * MIB),
        name="cycle",
    )(vmem(give), vmem(keep), coarse_diag.reshape(nc // bs, bs), x1, vmem(res), deg2, ids.reshape(-1), columns.T, block_counts, weights)
    return out.reshape(nb * bs, width)


def solution(mesh):
    both = ("rows", "cores")
    return jax.shard_map(
        functools.partial(body, mesh.shape["rows"], mesh.shape["cores"]),
        mesh=mesh,
        in_specs=(
            P(both, None), P(both, None), P(both), P(both, None, None, None), P(both, None),
            P(both), P(both, None, None), P(both), P(),
        ),
        out_specs=P(both, None),
        check_vma=False,
    )
```

time: 207 us -> 195 us (0.942)
  Pallas kernels: 204 us -> 193 us
  other arithmetic: 2.77 us -> 0 us
    pallas_call x3 -> x2, Pallas kernels: 89 us -> 81.9 us  [the longest x1 71.2 us: body(): pl.pallas_call(functools.partial(cycle_kernel, parts, stages), out_shape=...]
    pallas_call x1, Pallas kernels: 115 us -> 111 us  [body(): pl.pallas_call(functools.partial(relax_kernel, nr, nz), out_shape=(field,...]
where the time goes in v1:
time: 195 us; the launch traced here: 194 us
  Pallas kernels  193 us (99%)
    pallas_call x1, Pallas kernels, body(): pl.pallas_call(functools.partial(relax_kernel, nr, nz), out_shape=(field,...  111 us
    pallas_call x1, Pallas kernels, body(): pl.pallas_call(functools.partial(cycle_kernel, parts, stages), out_shape=...  71.2 us
    pallas_call x1, Pallas kernels, body(): pl.pallas_call(functools.partial(restrict_kernel, ways), out_shape=(pltpu...  10.6 us

profile of v1, /device:TPU:1, one launch (start us, length us, event | category | flops | bytes accessed | tf_op | source)
XLA Modules:
  0.0 194.3 jit_solution(2788093490099487041)
XLA Ops:
  0.0 0.0 copy-start
  0.0 111.1 %relax.1 = (f32[32,128,128]{2,1,0:T(8,128)}, f32[32,128,128]{2,1,0:T(8,128)S(1)}, s32[96,128]{1,0:T(8,128)}) custom-call(f32[32,128,128]{2,1,0:T(8,128)} %bitcast.15, f32[32,128,128]{2,1,0:T(8,128)} %bitcast.16, f32[32,128]{1,0:T(8,128)} %bitcast.18, s32[32,128]{1,0:T(8,128)} %bitcast.14, s32[16,32]{1,0:T(8,128)} %bitcast.21, s32[32]{0:T(128)} %counts.3, ...), custom_call_target="tpu_custom_call" | custom-call | tf_op jit(solution)/shard_map/relax/pallas_call | solution.py:471
  111.1 0.0 copy-done
  111.1 10.6 %restrict.1 = (f32[8192,128]{1,0:T(8,128)S(1)}, bf16[8192,128]{1,0:T(8,128)(2,1)S(1)}) custom-call(s32[4096]{0:T(1024)S(1)} %copy-done, f32[4096,128]{1,0:T(8,128)S(1)} %bitcast.13), custom_call_target="tpu_custom_call" | custom-call | tf_op jit(solution)/shard_map/restrict/pallas_call | solution.py:497
  121.8 71.2 %cycle.1 = f32[32,128,128]{2,1,0:T(8,128)S(1)} custom-call(bf16[8192,128]{1,0:T(8,128)(2,1)S(1)} %get-tuple-element.11.give, f32[8192,128]{1,0:T(8,128)S(1)} %get-tuple-element.12.keep, f32[128,128]{1,0:T(8,128)} %bitcast.17, f32[32,128,128]{2,1,0:T(8,128)} %get-tuple-element.13.x1_hbm, f32[32,128,128]{2,1,0:T(8,128)S(1)} %get-tuple-element.10.res, ...), custom_call_target="tpu_custom_call" | custom-call | tf_op jit(solution)/shard_map/cycle/pallas_call | solution.py:524
  193.0 1.3 copy.11
Async XLA Ops:
  0.0 111.1 %copy-start = (s32[4096]{0:T(1024)S(1)}, s32[4096]{0:T(1024)}, u32[]{:S(2)}) copy-start(s32[4096]{0:T(1024)} %agg.1) | copy-start | bytes 49156

commit v2 on v1

--- a/solution.py
+++ b/solution.py
@@ -59,10 +59,10 @@
             act(i * step + u)
 
 
-def relax_kernel(nr, nz, guess, rhs_hbm, deg, agg, cols, counts, sends, w_hbm,
+def relax_kernel(nr, nz, guess_hbm, rhs_hbm, deg, agg, cols, counts, sends, w_hbm,
                  x1_out, res, ids_out,
-                 w, tab1, tab2, pack, aggpack, hagg, dcol, rhs, x1, ex, pick, spot,
-                 wsem, bsem, xsem, s1, r1, s2, r2, sa, ra):
+                 w, guess, tab1, tab2, pack, aggpack, hagg, dcol, rhs, x1, ex, pick, spot,
+                 wsem, bsem, gsem, xsem, s1, r1, s2, r2, sa, ra):
     n = nr * nz
     nb, half = w.shape[0], w.shape[1] // 2
     mb = pack.shape[0] // n
@@ -78,6 +78,9 @@
 
     weights_copy = pltpu.make_async_copy(w_hbm, w, wsem)
     rhs_copy = pltpu.make_async_copy(rhs_hbm, rhs, bsem)
+    guess_copy = pltpu.make_async_copy(guess_hbm, guess, gsem)
+    guess_copy.start()
+    guess_copy.wait()
     weights_copy.start()
     rhs_copy.start()
 
@@ -177,6 +180,168 @@
     @pl.loop(1, n)
     def _(k):
         data_copy(k, tab2, s2, r2).wait_send()
+
+    x1_copy.wait()
+
+
+def split_kernel(nr, nz, guess_hbm, rhs_hbm, deg, agg, cols, counts, sends, w_hbm,
+                 x1_out, res, ids_out,
+                 w, guess, tab1a, tab1b, tab2a, tab2b, pack1a, pack1b, pack2a, pack2b,
+                 aggpack, hagg, dcol, rhs, x1, ex, pick, spot,
+                 wsem, bsem, gsem, xsem, s1a, r1a, s1b, r1b, s2a, r2a, s2b, r2b, sa, ra):
+    n = nr * nz
+    nb, half = w.shape[0], w.shape[1] // 2
+    middle = guess.shape[2] // 2
+    me = lax.axis_index("rows") * nz + lax.axis_index("cores")
+    barrier = pltpu.get_barrier_semaphore()
+    left = lax.broadcasted_iota(i32, guess.shape[1:], 1) < middle
+    trips = (
+        (tab1a, pack1a, s1a, r1a), (tab1b, pack1b, s1b, r1b),
+        (tab2a, pack2a, s2a, r2a), (tab2b, pack2b, s2b, r2b),
+    )
+
+    def where(t):
+        return (t // nz, lax.rem(t, nz))
+
+    def swap(block):
+        return pltpu.roll(block, middle, 1)
+
+    @pl.loop(1, n)
+    def _(k):
+        pl.semaphore_signal(barrier, 1, device_id=where(lax.rem(me + k, n)), device_id_type=MESH)
+
+    weights_copy = pltpu.make_async_copy(w_hbm, w, wsem)
+    rhs_copy = pltpu.make_async_copy(rhs_hbm, rhs, bsem)
+    guess_copy = pltpu.make_async_copy(guess_hbm, guess, gsem)
+    guess_copy.start()
+
+    def packed(field, side, t):
+        one, two = field[sends[0, t]], field[sends[1, t]]
+        return (jnp.where(left, one, swap(two)) if side == 0 else jnp.where(left, swap(one), two)).astype(bf16)
+
+    def data_copy(trip, k):
+        tab, pack, ss, rr = trips[trip]
+        t = lax.rem(me + k, n)
+        return pltpu.make_async_remote_copy(
+            src_ref=pack.at[t], dst_ref=tab.at[nb + me * 2 + trip % 2],
+            send_sem=ss.at[k], recv_sem=rr.at[k], device_id=where(t), device_id_type=MESH)
+
+    def send_all(trip):
+        @pl.loop(1, n)
+        def _(k):
+            data_copy(trip, k).start()
+
+    def take_all(trip):
+        tab, side = trips[trip][0], trip % 2
+        tab[nb + me * 2 + side] = trips[trip][1][me]
+
+        @pl.loop(1, n)
+        def _(k):
+            data_copy(trip, k).wait_recv()
+
+        @pl.loop(0, n)
+        def _(t):
+            tab[nb + t * 2 + 1 - side] = swap(tab[nb + t * 2 + side].astype(f32)).astype(bf16)
+
+    def agg_copy(k):
+        t = lax.rem(me + k, n)
+        return pltpu.make_async_remote_copy(
+            src_ref=aggpack.at[t], dst_ref=hagg.at[me],
+            send_sem=sa.at[k], recv_sem=ra.at[k], device_id=where(t), device_id_type=MESH)
+
+    guess_copy.wait()
+
+    @pl.loop(0, n)
+    def _(t):
+        pack1a[t] = packed(guess, 0, t)
+
+    pl.semaphore_wait(barrier, n - 1)
+    send_all(0)
+    weights_copy.start()
+    rhs_copy.start()
+
+    @pl.loop(0, n)
+    def _(t):
+        pack1b[t] = packed(guess, 1, t)
+        for j in range(2):
+            aggpack[t, pl.ds(j, 1), :] = agg[pl.ds(sends[j, t], 1), :]
+
+    send_all(1)
+
+    @pl.loop(1, n)
+    def _(k):
+        agg_copy(k).start()
+
+    hagg[me] = aggpack[me]
+
+    @pl.loop(0, nb)
+    def _(b):
+        block = guess[b].astype(bf16)
+        tab1a[b] = block
+        tab1b[b] = block
+        dcol[b] = column_of(deg, b)
+
+    find_full_rows(counts, half, pick, spot)
+    ex[pick.shape[0]] = jnp.zeros(ex.shape[1:], f32)
+    weights_copy.wait()
+    rhs_copy.wait()
+
+    def sweep(side):
+        tab = trips[side][0]
+
+        def act(b):
+            d, g = dcol[b], guess[b]
+            off = row_product(w, tab, cols, b, 0, half) + ex[spot[b]]
+            fresh = g + damping * (rhs[b] - (d * g - off)) / d
+            if side:
+                fresh = jnp.where(left, x1[b], fresh)
+            x1[b] = fresh
+            trips[2 + side][0][b] = fresh.astype(bf16)
+
+        take_all(side)
+        full_products(w, tab, cols, half, pick, ex)
+        each_row(nb, 8, act)
+        pack = trips[2 + side][1]
+
+        @pl.loop(0, n)
+        def _(t):
+            pack[t] = packed(x1, side, t)
+
+        send_all(2 + side)
+
+    sweep(0)
+    sweep(1)
+    x1_copy = pltpu.make_async_copy(x1, x1_out, xsem)
+    x1_copy.start()
+
+    @pl.loop(1, n)
+    def _(k):
+        agg_copy(k).wait()
+
+    ids_out[pl.ds(0, nb), :] = agg[...]
+
+    @pl.loop(0, n)
+    def _(t):
+        ids_out[pl.ds(nb + t * 2, 2), :] = hagg[t]
+
+    def residue(side):
+        tab = trips[2 + side][0]
+
+        def act(b):
+            off = row_product(w, tab, cols, b, 0, half) + ex[spot[b]]
+            fresh = rhs[b] - (dcol[b] * x1[b] - off)
+            res[b] = jnp.where(left, res[b], fresh) if side else fresh
+
+        take_all(2 + side)
+        full_products(w, tab, cols, half, pick, ex)
+        each_row(nb, 8, act)
+
+    residue(0)
+    residue(1)
+    for trip in range(4):
+        @pl.loop(1, n)
+        def _(k):
+            data_copy(trip, k).wait_send()
 
     x1_copy.wait()
 
@@ -452,7 +617,7 @@
     b = core + swapped + together
     c = core + apart + row_bits
     d = core + apart + swapped
-    return [(c, 2), (d, 2), (a, 6), (b, 6), (c, 2), (d, 2), (a, 6), (b, 6)]
+    return 4 * [(a, 3), (b, 3), (c, 1), (d, 1)]
 
 
 def body(nr, nz, rhs, guess, degree, weights, columns, block_counts, send_lists, aggregates, coarse_diag):
@@ -468,16 +633,21 @@
     deg2, agg2 = degree.reshape(nb, bs), aggregates.reshape(nb, bs)
     field = jax.ShapeDtypeStruct((nb, bs, width), f32)
 
+    table, message = pltpu.VMEM((nt, bs, width), bf16), pltpu.VMEM((n, bs, width), bf16)
+    split = mb == 2 and nt <= 4 * nb
+    if split:
+        kernel, tables, trips = split_kernel, [table] * 4 + [message] * 4, 4
+    else:
+        kernel, tables, trips = relax_kernel, [table] * 2 + [pltpu.VMEM((n * mb, bs, width), bf16)], 2
     x1, res, ids = pl.pallas_call(
-        functools.partial(relax_kernel, nr, nz),
+        functools.partial(kernel, nr, nz),
         out_shape=(field, pltpu.VMEM((nb, bs, width), f32), jax.ShapeDtypeStruct((nt, bs), i32)),
-        in_specs=[VM, ANY, VM, VM, SM, SM, SM, ANY],
+        in_specs=[ANY, ANY, VM, VM, SM, SM, SM, ANY],
         out_specs=(ANY, VM, VM),
         scratch_shapes=[
             pltpu.VMEM((nb, slots, bs, bs), bf16),
-            pltpu.VMEM((nt, bs, width), bf16),
-            pltpu.VMEM((nt, bs, width), bf16),
-            pltpu.VMEM((n * mb, bs, width), bf16),
+            pltpu.VMEM((nb, bs, width), f32),
+            *tables,
             pltpu.VMEM((n, mb, bs), i32),
             pltpu.VMEM((n, mb, bs), i32),
             pltpu.VMEM((nb, bs, width), f32),
@@ -485,7 +655,7 @@
             pltpu.VMEM((nb, bs, width), f32),
             pltpu.VMEM((extra + 1, bs, width), f32),
             pltpu.SMEM((extra,), i32), pltpu.SMEM((nb,), i32),
-            dma, dma, dma, dma((n,)), dma((n,)), dma((n,)), dma((n,)), dma((n,)), dma((n,)),
+            dma, dma, dma, dma, *[dma((n,))] * (2 * trips + 2),
         ],
         compiler_params=pltpu.CompilerParams(
             collective_id=1, has_side_effects=True, vmem_limit_bytes=54 * MIB),

time: 195 us -> 191 us (0.979)
  Pallas kernels: 193 us -> 190 us
    pallas_call x1, Pallas kernels: 71.2 us -> 68.3 us  [body(): pl.pallas_call(functools.partial(cycle_kernel, parts, stages), out_shape=...]
where the time goes in v2:
time: 191 us
  Pallas kernels  190 us (99%)
    pallas_call x1, Pallas kernels, body(): pl.pallas_call(functools.partial(kernel, nr, nz), out_shape=(field, pltpu...  111 us
    pallas_call x1, Pallas kernels, body(): pl.pallas_call(functools.partial(cycle_kernel, parts, stages), out_shape=...  68.3 us
    pallas_call x1, Pallas kernels, body(): pl.pallas_call(functools.partial(restrict_kernel, ways), out_shape=(pltpu...  10.6 us

profile of v2, /device:TPU:1, one launch (start us, length us, event | category | flops | bytes accessed | tf_op | source)
XLA Modules:
  0.0 191.2 jit_solution(2595912221249777247)
XLA Ops:
  0.0 0.0 copy-start
  0.0 110.9 %relax.1 = (f32[32,128,128]{2,1,0:T(8,128)}, f32[32,128,128]{2,1,0:T(8,128)S(1)}, s32[96,128]{1,0:T(8,128)}) custom-call(f32[32,128,128]{2,1,0:T(8,128)} %bitcast.15, f32[32,128,128]{2,1,0:T(8,128)} %bitcast.16, f32[32,128]{1,0:T(8,128)} %bitcast.18, s32[32,128]{1,0:T(8,128)} %bitcast.14, s32[16,32]{1,0:T(8,128)} %bitcast.21, s32[32]{0:T(128)} %counts.3, ...), custom_call_target="tpu_custom_call" | custom-call | tf_op jit(solution)/shard_map/relax/pallas_call | solution.py:642
  110.9 0.0 copy-done
  110.9 10.6 %restrict.1 = (f32[8192,128]{1,0:T(8,128)S(1)}, bf16[8192,128]{1,0:T(8,128)(2,1)S(1)}) custom-call(s32[4096]{0:T(1024)S(1)} %copy-done, f32[4096,128]{1,0:T(8,128)S(1)} %bitcast.13), custom_call_target="tpu_custom_call" | custom-call | tf_op jit(solution)/shard_map/restrict/pallas_call | solution.py:667
  121.6 68.3 %cycle.1 = f32[32,128,128]{2,1,0:T(8,128)S(1)} custom-call(bf16[8192,128]{1,0:T(8,128)(2,1)S(1)} %get-tuple-element.11.give, f32[8192,128]{1,0:T(8,128)S(1)} %get-tuple-element.12.keep, f32[128,128]{1,0:T(8,128)} %bitcast.17, f32[32,128,128]{2,1,0:T(8,128)} %get-tuple-element.13.x1_hbm, f32[32,128,128]{2,1,0:T(8,128)S(1)} %get-tuple-element.10.res, ...), custom_call_target="tpu_custom_call" | custom-call | tf_op jit(solution)/shard_map/cycle/pallas_call | solution.py:694
  189.9 1.3 copy.11
Async XLA Ops:
  0.0 110.9 %copy-start = (s32[4096]{0:T(1024)S(1)}, s32[4096]{0:T(1024)}, u32[]{:S(2)}) copy-start(s32[4096]{0:T(1024)} %agg.1) | copy-start | bytes 49156

commit v3 on v2

--- a/solution.py
+++ b/solution.py
@@ -382,8 +382,8 @@
 
 
 def cycle_kernel(parts, stages, give, keep, diag, x1_hbm, res, deg, ids_hbm, cols, counts, w_hbm, out,
-                 w, first, sbuf, rbuf, corr, fine, tab, ex, base, dcol, dinv, turned, ids, pick, spot,
-                 ss, rs, sg, rg, more):
+                 w, first, sbuf, rbuf, corr, fine, tab, ex, base, dcol, dinv, turned, pick, spot,
+                 ss, rs, sg, rg, more, *windows):
     top = keep.shape[0]
     acc = fine
     nb, half, size = w.shape[0], w.shape[1] // 2, w.shape[2]
@@ -427,10 +427,16 @@
                 if key not in met:
                     met.append(key)
                     pl.semaphore_signal(barrier, 1, device_id=peer(bits, d)[0], device_id_type=MESH)
-    pairs = ((ids_hbm, ids), (x1_hbm, base), (w_hbm, w))
-    others = [pltpu.make_async_copy(a, b, more.at[k]) for k, (a, b) in enumerate(pairs)]
+    others = [pltpu.make_async_copy(a, b, more.at[k]) for k, (a, b) in enumerate(((x1_hbm, base), (w_hbm, w)))]
     others[0].start()
-    others[1].start()
+    span = windows[0].shape[0]
+
+    def fetch(i, k):
+        part = pl.ds((i * len(windows) + k) * span, span)
+        return pltpu.make_async_copy(ids_hbm.at[part], windows[k], more.at[2 + k])
+
+    for k in range(len(windows)):
+        fetch(0, k).start()
     pl.semaphore_wait(barrier, len(met))
 
     room, slots, at, taken = {}, {}, 0, 0
@@ -524,13 +530,13 @@
                 hop(p, s, d).start()
             regions[p], sizes[p] = regions[p] + peer(bits, 0)[1] * left, left
         if s == 1:
-            others[2].start()
+            others[1].start()
 
             @pl.loop(0, nb)
             def _(b):
                 dcol[b] = damping / column_of(deg, b)
 
-            others[1].wait()
+            others[0].wait()
 
             @pl.loop(0, nb)
             def _(b):
@@ -579,7 +585,6 @@
             sent += waits[p]
             if s == 0:
                 widen(shift + begin[p], parts[p])
-    others[0].wait()
     for p in range(count):
         for copy in waits[p]:
             copy.wait_recv()
@@ -587,13 +592,24 @@
 
     step = 16
 
-    @pl.loop(0, tab.shape[0])
-    def _(b):
-        for i in range(size // step):
-            tab[b, i * step:(i + 1) * step, :] = jnp.concatenate(
-                [fine[pl.ds(ids[b * size + i * step + u], 1), :] for u in range(step)], axis=0).astype(bf16)
-
-    others[2].wait()
+    blocks = span // size
+    rounds = tab.shape[0] // (blocks * len(windows))
+
+    @pl.loop(0, rounds)
+    def _(i):
+        for k, window in enumerate(windows):
+            fetch(i, k).wait()
+            for q in range(blocks):
+                b = (i * len(windows) + k) * blocks + q
+                for at in range(0, size, step):
+                    tab[b, at:at + step, :] = jnp.concatenate(
+                        [fine[pl.ds(window[q * size + at + u], 1), :] for u in range(step)], axis=0).astype(bf16)
+
+            @pl.when(i + 1 < rounds)
+            def _():
+                fetch(i + 1, k).start()
+
+    others[1].wait()
     full_products(w, tab, cols, half, pick, ex)
 
     def finish(b):
@@ -709,8 +725,9 @@
             pltpu.VMEM((nb, bs, width), f32),
             pltpu.VMEM((top // (n // 2), width), f32),
             pltpu.VMEM((bs, width), f32),
-            pltpu.SMEM((nt * bs,), i32), pltpu.SMEM((extra,), i32), pltpu.SMEM((nb,), i32),
-            dma((hops,)), dma((hops,)), dma((hops,)), dma((hops,)), dma((3,)),
+            pltpu.SMEM((extra,), i32), pltpu.SMEM((nb,), i32),
+            dma((hops,)), dma((hops,)), dma((hops,)), dma((hops,)), dma((10,)),
+            *[pltpu.SMEM((2 * bs,), i32)] * 8,
         ],
         compiler_params=pltpu.CompilerParams(
             collective_id=2, has_side_effects=True, vmem_limit_bytes=52 * MIB if nt > 128 else 46 * MIB),

time: 191 us -> 188 us (0.984)
  Pallas kernels: 190 us -> 187 us
    pallas_call x1, Pallas kernels: 68.3 us -> 65.3 us  [body(): pl.pallas_call(functools.partial(cycle_kernel, parts, stages), out_shape=...]
where the time goes in v3:
time: 188 us
  Pallas kernels  187 us (99%)
    pallas_call x1, Pallas kernels, body(): pl.pallas_call(functools.partial(kernel, nr, nz), out_shape=(field, pltpu...  111 us
    pallas_call x1, Pallas kernels, body(): pl.pallas_call(functools.partial(cycle_kernel, parts, stages), out_shape=...  65.3 us
    pallas_call x1, Pallas kernels, body(): pl.pallas_call(functools.partial(restrict_kernel, ways), out_shape=(pltpu...  10.6 us

profile of v3, /device:TPU:1, one launch (start us, length us, event | category | flops | bytes accessed | tf_op | source)
XLA Modules:
  0.0 188.2 jit_solution(5754267852857744899)
XLA Ops:
  0.0 0.0 copy-start
  0.0 110.9 %relax.1 = (f32[32,128,128]{2,1,0:T(8,128)}, f32[32,128,128]{2,1,0:T(8,128)S(1)}, s32[96,128]{1,0:T(8,128)}) custom-call(f32[32,128,128]{2,1,0:T(8,128)} %bitcast.15, f32[32,128,128]{2,1,0:T(8,128)} %bitcast.16, f32[32,128]{1,0:T(8,128)} %bitcast.18, s32[32,128]{1,0:T(8,128)} %bitcast.14, s32[16,32]{1,0:T(8,128)} %bitcast.21, s32[32]{0:T(128)} %counts.3, ...), custom_call_target="tpu_custom_call" | custom-call | tf_op jit(solution)/shard_map/relax/pallas_call | solution.py:658
  110.9 0.0 copy-done
  110.9 10.6 %restrict.1 = (f32[8192,128]{1,0:T(8,128)S(1)}, bf16[8192,128]{1,0:T(8,128)(2,1)S(1)}) custom-call(s32[4096]{0:T(1024)S(1)} %copy-done, f32[4096,128]{1,0:T(8,128)S(1)} %bitcast.13), custom_call_target="tpu_custom_call" | custom-call | tf_op jit(solution)/shard_map/restrict/pallas_call | solution.py:683
  121.6 65.3 %cycle.1 = f32[32,128,128]{2,1,0:T(8,128)S(1)} custom-call(bf16[8192,128]{1,0:T(8,128)(2,1)S(1)} %get-tuple-element.11.give, f32[8192,128]{1,0:T(8,128)S(1)} %get-tuple-element.12.keep, f32[128,128]{1,0:T(8,128)} %bitcast.17, f32[32,128,128]{2,1,0:T(8,128)} %get-tuple-element.13.x1_hbm, f32[32,128,128]{2,1,0:T(8,128)S(1)} %get-tuple-element.10.res, ...), custom_call_target="tpu_custom_call" | custom-call | tf_op jit(solution)/shard_map/cycle/pallas_call | solution.py:710
  186.9 1.3 copy.11
Async XLA Ops:
  0.0 110.9 %copy-start = (s32[4096]{0:T(1024)S(1)}, s32[4096]{0:T(1024)}, u32[]{:S(2)}) copy-start(s32[4096]{0:T(1024)} %agg.1) | copy-start | bytes 49156
